TPU v7x, 32 devices: a whole 2x2x4 slice. The times are simulated.
32 devices in a mesh: row: 4 (over y, x), col: 4 (over z), depth: 2 (over core).
Axes of the slice: x: 2, y: 2, z: 4, core: 2. Of those that a mesh axis runs over, the one named last changes fastest.
Arguments:
- matrix_columns: float32 [4, 8, 768, 24576], P(None, ('col', 'depth'), None, 'row'), may hold values from -0.0390625 to 0.0390625
- sources: float32 [4, 8, 768, 128], P('row', ('col', 'depth')), may hold values from -6 to 6
Outputs:
- first_image: float32 [4, 8, 768, 128], P('row', ('col', 'depth'))
- second_image: float32 [4, 8, 768, 128], P('row', ('col', 'depth'))
All inputs are finite; a program needn't handle non-finite values.
Results may differ from a plain program's by a relative error of at most 0.00011.
Values sent between devices are 32-bit elements; how exact they have to be, the bound alone decides.
A program may use at most 128 MiB of HBM per device.

v0:
```python
import jax
import jax.numpy as jnp
from jax import lax
from jax.sharding import PartitionSpec as P


def contract(window, inputs_flat):
    return lax.dot_general(
        window,
        inputs_flat,
        (((0,), (0,)), ((), ())),
        precision=lax.Precision.HIGHEST,
        preferred_element_type=jnp.float32,
    )


def apply_once(columns, vector_part):
    piece_len = vector_part.shape[2]
    width = vector_part.shape[3]
    gathered = lax.all_gather(vector_part, "row", axis=0, tiled=True)
    inputs_flat = gathered.reshape(-1, width)
    owned = lax.psum_scatter(
        contract(columns, inputs_flat), ("col", "depth"), scatter_dimension=0, tiled=True
    )
    return owned.reshape(1, 1, piece_len, width)


def body(matrix_columns, sources):
    rows_here = matrix_columns.shape[3]
    columns = matrix_columns.reshape(-1, rows_here)
    first_image = apply_once(columns, sources)
    second_image = apply_once(columns, first_image)
    return (first_image, second_image)


def solution(mesh):
    in_specs = (P(None, ("col", "depth"), None, "row"), P("row", ("col", "depth"), None, None))
    out_specs = (P("row", ("col", "depth"), None, None), P("row", ("col", "depth"), None, None))
    return jax.shard_map(body, mesh=mesh, in_specs=in_specs, out_specs=out_specs, check_vma=False)
```

profile of v0, /device:TPU:0, one launch (start us, length us, event | category | flops | bytes accessed | tf_op | source)
XLA Modules:
  0.0 336.2 jit_solution(16498725808453203450)
XLA Ops:
  7.2 0.0 all-gather.4.cloned.1.call-start
  7.2 0.7 all-gather.4.cloned.1.call-update
  7.9 0.0 reduce-scatter.3.cloned.1.call-start
  7.9 35.5 %all-gather.4.cloned.1.call-done = f32[4,1,768,128]{3,2,1,0:T(8,128)} async-done(((f32[1,1,768,128]{3,2,1,0:T(8,128)}), f32[4,1,768,128]{3,2,1,0:T(8,128)}) %all-gather.4.cloned.1.call-update) | async-done | bytes 1572880 | tf_op jit(solution)/shard_map/all_gather | solution.py:20
  43.4 123.5 %fusion.4 = f32[6144,128]{1,0:T(8,128)} fusion(f32[4,1,768,6144]{3,2,1,0:T(8,128)} %param.2, f32[4,1,768,128]{3,2,1,0:T(8,128)} %all-gather.4.cloned.1.call-done), kind=kOutput, calls=%fused_computation.4 | convolution fusion | flops 28991029248 | bytes 80216064 | tf_op jit(solution)/shard_map/dot_general | solution.py:8
  166.9 0.0 reduce-scatter.3.cloned.1.call-update
  166.9 0.0 all-gather.6.cloned.1.call-start
  166.9 40.5 %reduce-scatter.3.cloned.1.call-done = f32[768,128]{1,0:T(8,128)} async-done(((f32[6144,128]{1,0:T(8,128)}), f32[768,128]{1,0:T(8,128)}) %reduce-scatter.3.cloned.1.call-update) | async-done | bytes 393232 | tf_op jit(solution)/shard_map/reduce_scatter | solution.py:22
  207.4 0.0 all-gather.6.cloned.1.call-update
  207.4 0.0 reduce-scatter.5.cloned.1.call-start
  207.5 32.4 %all-gather.6.cloned.1.call-done = f32[3072,128]{1,0:T(8,128)} async-done(((f32[768,128]{1,0:T(8,128)}), f32[3072,128]{1,0:T(8,128)}) %all-gather.6.cloned.1.call-update) | async-done | bytes 1572880 | tf_op jit(solution)/shard_map/all_gather | solution.py:20
  239.8 47.4 %fusion.7 = f32[6144,128]{0,1:T(8,128)} fusion(f32[4,768,128]{2,1,0:T(8,128)} %bitcast.22, f32[4,1,768,6144]{3,2,1,0:T(8,128)} %param.2), kind=kOutput, calls=%fused_computation.5 | convolution fusion | flops 28991029248 | bytes 80216064 | tf_op jit(solution)/shard_map/dot_general | solution.py:8
  287.2 0.0 reduce-scatter.5.cloned.1.call-update
  287.2 40.5 %reduce-scatter.5.cloned.1.call-done = f32[768,128]{0,1:T(8,128)} async-done(((f32[6144,128]{0,1:T(8,128)}), f32[768,128]{0,1:T(8,128)}) %reduce-scatter.5.cloned.1.call-update) | async-done | bytes 393232 | tf_op jit(solution)/shard_map/reduce_scatter | solution.py:22
  327.8 1.9 copy.10
Async XLA Ops:
  7.2 36.2 %all-gather.4.cloned.1.call-start = ((), (), s32[]{:S(2)}) async-start(), calls=%async_computation.2 | async-start | bytes 1966080 | tf_op jit(solution)/shard_map/all_gather | solution.py:20
  7.9 199.5 %reduce-scatter.3.cloned.1.call-start = ((), (), s32[]{:S(2)}) async-start(), calls=%async_computation.3 | async-start | bytes 3538944 | tf_op jit(solution)/shard_map/reduce_scatter | solution.py:22
  166.9 73.0 %all-gather.6.cloned.1.call-start = ((), (), s32[]{:S(2)}) async-start(), calls=%async_computation.5 | async-start | bytes 1966080 | tf_op jit(solution)/shard_map/all_gather | solution.py:20
  207.4 120.3 %reduce-scatter.5.cloned.1.call-start = ((), (), s32[]{:S(2)}) async-start(), calls=%async_computation.4 | async-start | bytes 3538944 | tf_op jit(solution)/shard_map/reduce_scatter | solution.py:22
Sparse Core Ops, SparseCore 0:
  9.8 33.5 all-gather.3
  167.0 40.3 reduce-scatter.2
  209.8 29.9 all-gather.5
  287.4 40.3 reduce-scatter.4
where the time goes:
time: 336 us
  matrix products  171 us (51%)
  waiting for transfers between devices  150 us (45%)
  between operations  13.8 us (4%)
    dot_general x2, matrix products, contract(): lax.dot_general(window, inputs_flat, (((0,), (0,)), ((), ())), precision=...  171 us
    reduce_scatter x2, waiting for transfers between devices, apply_once(): lax.psum_scatter(contract(columns, inputs_flat), ('col', 'depth'), scatte...  81 us
    all_gather x2, waiting for transfers between devices, apply_once(): gathered = lax.all_gather(vector_part, 'row', axis=0, tiled=True)  67.8 us
  transfers between devices with their start and end apart: 4, of which 4 were waited for; matrix products, arithmetic and copies ran while one was open for 0% of the time, Pallas kernels for 0%

commit v1 on v0

v1 whole, which is shorter than its diff:
```python
import functools

import jax
import jax.numpy as jnp
from jax import lax
from jax.experimental import pallas as pl
from jax.experimental.pallas import tpu as pltpu
from jax.sharding import PartitionSpec as P

LANES = 256


def split(values):
    high = values.astype(jnp.bfloat16)
    low = (values - high.astype(jnp.float32)).astype(jnp.bfloat16)
    return high, low


def product_kernel(x_ref, a_ref, out_ref, xt_ref):
    width = x_ref.shape[1]
    depth = x_ref.shape[0]
    tile = a_ref.shape[3]

    @pl.when(pl.program_id(0) == 0)
    def _():
        high, low = split(x_ref[...].T)
        xt_ref[:width, :] = high
        xt_ref[width:, :] = low

    for start in range(0, tile, LANES):
        block = a_ref[:, 0, :, start:start + LANES].reshape(depth, LANES)
        high, low = split(block)
        main = jnp.dot(xt_ref[...], high, preferred_element_type=jnp.float32)
        rest = jnp.dot(xt_ref[:width, :], low, preferred_element_type=jnp.float32)
        total = main[:width] + (main[width:] + rest)
        out_ref[start:start + LANES, :] = total.T


def product(columns, inputs_flat):
    outer, _, piece, rows = columns.shape
    depth, width = inputs_flat.shape
    tile = 2 * LANES
    return pl.pallas_call(
        product_kernel,
        grid=(rows // tile,),
        out_shape=jax.ShapeDtypeStruct((rows, width), jnp.float32),
        in_specs=[
            pl.BlockSpec((depth, width), lambda i: (0, 0)),
            pl.BlockSpec((outer, 1, piece, tile), lambda i: (0, 0, 0, i)),
        ],
        out_specs=pl.BlockSpec((tile, width), lambda i: (i, 0)),
        scratch_shapes=[pltpu.VMEM((2 * width, depth), jnp.bfloat16)],
        compiler_params=pltpu.CompilerParams(
            dimension_semantics=("arbitrary",), vmem_limit_bytes=48 << 20
        ),
        cost_estimate=pl.CostEstimate(
            flops=6 * rows * depth * width, bytes_accessed=4 * rows * depth, transcendentals=0
        ),
    )(inputs_flat, columns)


def apply_once(columns, vector_part):
    piece_len = vector_part.shape[2]
    width = vector_part.shape[3]
    gathered = lax.all_gather(vector_part, "row", axis=0, tiled=True)
    inputs_flat = gathered.reshape(-1, width)
    owned = lax.psum_scatter(
        product(columns, inputs_flat), ("col", "depth"), scatter_dimension=0, tiled=True
    )
    return owned.reshape(1, 1, piece_len, width)


def body(matrix_columns, sources):
    first_image = apply_once(matrix_columns, sources)
    second_image = apply_once(matrix_columns, first_image)
    return (first_image, second_image)


def solution(mesh):
    in_specs = (P(None, ("col", "depth"), None, "row"), P("row", ("col", "depth"), None, None))
    out_specs = (P("row", ("col", "depth"), None, None), P("row", ("col", "depth"), None, None))
    return jax.shard_map(body, mesh=mesh, in_specs=in_specs, out_specs=out_specs, check_vma=False)
```

time: 336 us -> 230 us (0.68)
  matrix products: 171 us -> 0 us
  Pallas kernels: 0 us -> 62.5 us
    dot_general x2 -> x0, matrix products: 171 us -> none  [contract(): lax.dot_general(window, inputs_flat, (((0,), (0,)), ((), ())), precision=...]
    pallas_call x0 -> x2, Pallas kernels: none -> 62.5 us  [product(): pl.pallas_call(product_kernel, grid=(rows // tile,), out_shape=jax.ShapeD...]
where the time goes in v1:
time: 230 us; the launch traced here: 229 us
  waiting for transfers between devices  150 us (65%)
  Pallas kernels  62.5 us (27%)
  between operations  13.8 us (6%)
  local copies, waits for them, and re-layouts  2.81 us (1%)
    reduce_scatter x2, waiting for transfers between devices, apply_once(): lax.psum_scatter(product(columns, inputs_flat), ('col', 'depth'), scatter...  81 us
    all_gather x2, waiting for transfers between devices, apply_once(): gathered = lax.all_gather(vector_part, 'row', axis=0, tiled=True)  67.9 us
    pallas_call x2, Pallas kernels, product(): pl.pallas_call(product_kernel, grid=(rows // tile,), out_shape=jax.ShapeD...  62.5 us
  transfers between devices with their start and end apart: 4, of which 4 were waited for; matrix products, arithmetic and copies ran while one was open for 0% of the time, Pallas kernels for 0%

profile of v1, /device:TPU:0, one launch (start us, length us, event | category | flops | bytes accessed | tf_op | source)
XLA Modules:
  0.0 228.9 jit_solution(8209069307372079450)
XLA Ops:
  7.2 0.0 all-gather.4.cloned.1.call-start
  7.2 0.7 all-gather.4.cloned.1.call-update
  7.9 0.0 reduce-scatter.3.cloned.1.call-start
  7.9 35.5 %all-gather.4.cloned.1.call-done = f32[4,1,768,128]{3,2,1,0:T(8,128)} async-done(((f32[1,1,768,128]{3,2,1,0:T(8,128)}), f32[4,1,768,128]{3,2,1,0:T(8,128)}) %all-gather.4.cloned.1.call-update) | async-done | bytes 1572880 | tf_op jit(solution)/shard_map/all_gather | solution.py:65
  43.4 0.0 copy-start
  43.4 1.4 copy-done
  44.8 31.3 %shard_map.41 = f32[6144,128]{1,0:T(8,128)} custom-call(f32[3072,128]{1,0:T(8,128)S(1)} %bitcast.3, f32[4,1,768,6144]{3,2,1,0:T(8,128)} %a_ref.3), custom_call_target="tpu_custom_call" | custom-call | flops 14495514624 | bytes 75497472 | tf_op jit(solution)/shard_map/pallas_call | solution.py:43
  76.1 0.0 reduce-scatter.3.cloned.1.call-update
  76.1 0.0 all-gather.6.cloned.1.call-start
  76.1 40.5 %reduce-scatter.3.cloned.1.call-done = f32[768,128]{1,0:T(8,128)} async-done(((f32[6144,128]{1,0:T(8,128)}), f32[768,128]{1,0:T(8,128)}) %reduce-scatter.3.cloned.1.call-update) | async-done | bytes 393232 | tf_op jit(solution)/shard_map/reduce_scatter | solution.py:67
  116.6 0.0 all-gather.6.cloned.1.call-update
  116.6 0.0 reduce-scatter.5.cloned.1.call-start
  116.7 32.4 %all-gather.6.cloned.1.call-done.x_ref = f32[3072,128]{1,0:T(8,128)} async-done(((f32[768,128]{1,0:T(8,128)}), f32[3072,128]{1,0:T(8,128)}) %all-gather.6.cloned.1.call-update) | async-done | bytes 1572880 | tf_op jit(solution)/shard_map/all_gather | solution.py:65
  149.1 0.0 copy-start.1
  149.1 1.4 copy-done.1
  150.5 31.3 %shard_map.42 = f32[6144,128]{1,0:T(8,128)} custom-call(f32[3072,128]{1,0:T(8,128)S(1)} %copy-done.1, f32[4,1,768,6144]{3,2,1,0:T(8,128)} %a_ref.3), custom_call_target="tpu_custom_call" | custom-call | flops 14495514624 | bytes 75497472 | tf_op jit(solution)/shard_map/pallas_call | solution.py:43
  181.8 0.0 reduce-scatter.5.cloned.1.call-update
  181.8 40.5 %reduce-scatter.5.cloned.1.call-done = f32[768,128]{1,0:T(8,128)} async-done(((f32[6144,128]{1,0:T(8,128)}), f32[768,128]{1,0:T(8,128)}) %reduce-scatter.5.cloned.1.call-update) | async-done | bytes 393232 | tf_op jit(solution)/shard_map/reduce_scatter | solution.py:67
Async XLA Ops:
  7.2 36.2 %all-gather.4.cloned.1.call-start = ((), (), s32[]{:S(2)}) async-start(), calls=%async_computation.2 | async-start | bytes 1966080 | tf_op jit(solution)/shard_map/all_gather | solution.py:65
  7.9 108.7 %reduce-scatter.3.cloned.1.call-start = ((), (), s32[]{:S(2)}) async-start(), calls=%async_computation.3 | async-start | bytes 3538944 | tf_op jit(solution)/shard_map/reduce_scatter | solution.py:67
  43.4 1.4 copy-start
  76.1 73.0 %all-gather.6.cloned.1.call-start = ((), (), s32[]{:S(2)}) async-start(), calls=%async_computation.5 | async-start | bytes 1966080 | tf_op jit(solution)/shard_map/all_gather | solution.py:65
  116.6 105.7 %reduce-scatter.5.cloned.1.call-start = ((), (), s32[]{:S(2)}) async-start(), calls=%async_computation.4 | async-start | bytes 3538944 | tf_op jit(solution)/shard_map/reduce_scatter | solution.py:67
  149.1 1.4 copy-start.1
Sparse Core Ops, SparseCore 0:
  9.8 33.5 all-gather.3
  76.2 40.3 reduce-scatter.2
  119.0 30.0 all-gather.5
  181.9 40.3 reduce-scatter.4
